TPU v7x, 32 devices: a whole 2x2x4 slice. The times are simulated.
32 devices in a mesh: ctx: 16 (over z, y, x), tp: 2 (over core).
Axes of the slice: x: 2, y: 2, z: 4, core: 2. Of those that a mesh axis runs over, the one named last changes fastest.
Arguments:
- queries: bfloat16 [1024, 2560], P('ctx', 'tp'), may hold values from -100 to 100
- projected_keys: bfloat16 [1024, 512], P('ctx', 'tp'), may hold values from -30 to 30
- projected_values: bfloat16 [1024, 512], P('ctx', 'tp'), may hold values from -6 to 6
- hidden: bfloat16 [1024, 5120], P('ctx', 'tp'), may hold values from -6 to 6
- route_ids: int32 [1024, 1], P('ctx'), may hold values from 0 to 15; in each aligned block of 64 rows (0 to 63, 64 to 127, ...) at most 6 rows name the same one
- route_gain: float32 [1024], P('ctx'), may hold values from 0.25 to 1
- w_gate: bfloat16 [16, 5120, 4096], P('ctx', None, 'tp'), may hold values from -0.078125 to 0.078125
- w_up: bfloat16 [16, 5120, 4096], P('ctx', None, 'tp'), may hold values from -0.078125 to 0.078125
- w_down: bfloat16 [16, 4096, 5120], P('ctx', None, 'tp'), may hold values from -0.09375 to 0.09375
Outputs:
- attended: bfloat16 [1024, 2560], P('ctx', 'tp')
- mixed: bfloat16 [1024, 5120], P('ctx', 'tp')
Inputs may be any that keep to these rules, and one draw needn't show every extreme that they name: `route_ids`: within the rows of one device (aligned blocks of 64 rows) no expert is named more than 6 times, a bound that some block reaches.
All inputs are finite; a program needn't handle non-finite values.
Results may differ from a plain program's by a relative error of at most 0.0057.
Values may be sent and summed in bfloat16 or wider, within the bound.
No kernel may reach another device: no remote copies, remote signals or barrier semaphores. Data moves between devices by JAX's collectives and lax.ppermute only.
A program may use at most 128 MiB of HBM per device.

v0:
```python
import math
import jax
import jax.numpy as jnp
from jax import lax
from jax.sharding import PartitionSpec as P

HEAD_SIZE = 128
EXPERTS = 16
CAP = 6
masked_score = -1e30


def body(
    queries, projected_keys, projected_values, hidden, route_ids, route_gain, w_gate, w_up, w_down
):
    tok_rows = queries.shape[0]
    width_q = queries.shape[1]
    width_kv = projected_keys.shape[1]
    ctx_count = lax.axis_size("ctx")
    ctx_index = lax.axis_index("ctx")
    offsets = jnp.arange(tok_rows, dtype=jnp.int32)
    query_use, key_use, value_use = (queries, projected_keys, projected_values)

    def position(device, offset):
        return device * tok_rows + offset

    query_pos = position(ctx_index, offsets)
    query_top = jnp.max(query_pos)
    kv_heads = width_kv // HEAD_SIZE
    head_group = width_q // HEAD_SIZE // kv_heads
    query_tensor = query_use.reshape(tok_rows, kv_heads, head_group, HEAD_SIZE)
    score_scale = HEAD_SIZE ** (-0.5)
    key_whole, value_whole = (
        lax.all_gather(key_use, "ctx", axis=0, tiled=True),
        lax.all_gather(value_use, "ctx", axis=0, tiled=True),
    )
    total_rows = key_whole.shape[0]
    block_rows = math.gcd(total_rows, 1024)

    def absorb_block(block_index, state):
        block_start = block_index * block_rows
        key_block = lax.dynamic_slice_in_dim(key_whole, block_start, block_rows, 0).reshape(
            block_rows, kv_heads, HEAD_SIZE
        )
        value_block = lax.dynamic_slice_in_dim(value_whole, block_start, block_rows, 0).reshape(
            block_rows, kv_heads, HEAD_SIZE
        )
        global_rows = block_start + jnp.arange(block_rows, dtype=jnp.int32)
        key_pos = position(global_rows // tok_rows, global_rows % tok_rows)

        def update(inner_state):
            running_max, running_sum, running_out = inner_state
            scores = (
                jnp.einsum(
                    "qhgd,khd->hgqk", query_tensor, key_block, preferred_element_type=jnp.float32
                )
                * score_scale
            )
            allowed = query_pos[:, None] >= key_pos[None, :]
            scores = jnp.where(allowed, scores, masked_score)
            new_max = jnp.maximum(running_max, jnp.max(scores, axis=3))
            weights = jnp.where(allowed, jnp.exp(scores - new_max[..., None]), 0.0)
            factor = jnp.exp(running_max - new_max)
            new_sum = running_sum * factor + jnp.sum(weights, axis=3)
            partial_out = jnp.einsum(
                "hgqk,khd->qhgd",
                weights.astype(jnp.bfloat16),
                value_block,
                preferred_element_type=jnp.float32,
            )
            new_out = running_out * jnp.transpose(factor, (2, 0, 1))[..., None] + partial_out
            return (new_max, new_sum, new_out)

        def keep_state(inner_state):
            return inner_state

        return lax.cond(jnp.min(key_pos) <= query_top, update, keep_state, state)

    initial = (
        jnp.full((kv_heads, head_group, tok_rows), masked_score, jnp.float32),
        jnp.zeros((kv_heads, head_group, tok_rows), jnp.float32),
        jnp.zeros((tok_rows, kv_heads, head_group, HEAD_SIZE), jnp.float32),
    )
    running_max, running_sum, running_out = lax.fori_loop(
        0, total_rows // block_rows, absorb_block, initial
    )
    attended = (
        (running_out / jnp.transpose(running_sum, (2, 0, 1))[..., None])
        .reshape(tok_rows, width_q)
        .astype(jnp.bfloat16)
    )
    ids_flat = route_ids[:, 0]
    chosen = (ids_flat[:, None] == jnp.arange(EXPERTS, dtype=jnp.int32)[None, :]).astype(jnp.int32)
    ranking = jnp.sum((jnp.cumsum(chosen, axis=0) - chosen) * chosen, axis=1)
    slot_of = ids_flat * CAP + ranking
    selector = (jnp.arange(EXPERTS * CAP, dtype=jnp.int32)[:, None] == slot_of[None, :]).astype(
        jnp.bfloat16
    )
    host_count = ctx_count // EXPERTS
    feature_width = hidden.shape[1]
    packed = jnp.dot(selector, hidden, preferred_element_type=jnp.float32).astype(jnp.bfloat16)
    packed = jnp.broadcast_to(
        packed.reshape(EXPERTS, 1, CAP, feature_width), (EXPERTS, host_count, CAP, feature_width)
    ).reshape(ctx_count, CAP, feature_width)
    arrived = lax.all_to_all(packed, "ctx", split_axis=0, concat_axis=0, tiled=True)
    arrived = lax.all_gather(arrived, "tp", axis=2, tiled=True)
    slot_count = arrived.shape[1]
    flat_rows = arrived.reshape(-1, arrived.shape[2])
    gate_val = jnp.dot(flat_rows, w_gate[0], preferred_element_type=jnp.float32)
    up_val = jnp.dot(flat_rows, w_up[0], preferred_element_type=jnp.float32)
    inner = (jax.nn.silu(gate_val) * up_val).astype(jnp.bfloat16)
    pair_inner = lax.all_gather(inner, "tp", axis=1, tiled=True)
    partial_out = jnp.dot(pair_inner, w_down[0], preferred_element_type=jnp.float32).astype(
        jnp.bfloat16
    )
    partial_out = partial_out.reshape(ctx_count, slot_count, partial_out.shape[1])
    returned = lax.all_to_all(partial_out, "ctx", split_axis=0, concat_axis=0, tiled=True)
    out_width = returned.shape[2]
    summed = returned.reshape(EXPERTS, host_count, CAP, out_width).astype(jnp.float32).sum(axis=1)
    summed = summed.reshape(EXPERTS * CAP, out_width)
    mixed = (summed[slot_of] * route_gain[:, None]).astype(jnp.bfloat16)
    return (attended, mixed)


def solution(mesh):
    in_specs = (
        P("ctx", "tp"),
        P("ctx", "tp"),
        P("ctx", "tp"),
        P("ctx", "tp"),
        P("ctx", None),
        P("ctx"),
        P("ctx", None, "tp"),
        P("ctx", None, "tp"),
        P("ctx", None, "tp"),
    )
    out_specs = (P("ctx", "tp"), P("ctx", "tp"))
    return jax.shard_map(body, mesh=mesh, in_specs=in_specs, out_specs=out_specs, check_vma=False)
```

profile of v0, /device:TPU:0, one launch (start us, length us, event | category | flops | bytes accessed | tf_op | source)
XLA Modules:
  0.0 152.1 jit_solution(1355597205857069275)
XLA Ops:
  0.6 0.0 copy-start
  0.7 0.8 fusion.35
  1.4 0.1 reduce_window_sum.11
  1.5 0.8 select_reduce_fusion
  2.4 0.7 multiply_add_fusion.1
  3.0 0.0 copy-done
  3.0 0.3 convolution_convert_fusion
  3.3 1.0 reshape_reshape.3
  4.3 8.3 %all-to-all-start = ((bf16[16,6,2560]{2,1,0:T(8,128)(2,1)}), bf16[16,6,2560]{2,1,0:T(8,128)(2,1)S(1)}, u32[]{:S(2)}, u32[]{:S(2)}) async-start(bf16[16,6,2560]{2,1,0:T(8,128)(2,1)} %reshape_reshape.3), calls=%async_computation | async-start | bytes 1310720 | tf_op jit(solution)/shard_map/all_to_all | solution.py:105
  12.7 0.6 fusion.48
  13.3 0.6 fusion.46
  15.3 0.0 copy-done.4
  15.3 45.2 %all_gather.12 = bf16[1024,256]{1,0:T(8,128)(2,1)S(1)} all-gather(bf16[64,256]{1,0:T(8,128)(2,1)S(1)} %copy-done.4), channel_id=1, replica_groups=mesh['ctx'=16,'tp'=2] {'ctx'}, dimensions={0}, use_global_device_ids=true | all-gather | bytes 557056 | tf_op jit(solution)/shard_map/all_gather | solution.py:34
  60.5 0.0 all-to-all-done
  60.5 2.7 %all_gather.14 = bf16[16,6,5120]{2,1,0:T(8,128)(2,1)S(1)} all-gather(bf16[16,6,2560]{2,1,0:T(8,128)(2,1)S(1)} %all-to-all-done), channel_id=1, replica_groups=mesh['ctx'=16,'tp'=2] {'tp'}, dimensions={2}, use_global_device_ids=true | all-gather | bytes 1474560 | tf_op jit(solution)/shard_map/all_gather | solution.py:106
  63.3 0.4 reshape.55
  63.6 0.0 slice-start
  63.6 0.0 slice-start.1
  63.7 0.0 slice-start.2
  63.7 8.9 %fusion.24 = f32[96,2048]{1,0:T(8,128)S(1)} fusion(bf16[96,5120]{1,0:T(8,128)(2,1)S(1)} %reshape.55, bf16[1,5120,2048]{2,1,0:T(8,128)(2,1)} %param.17), kind=kOutput, calls=%fused_computation.26 | convolution fusion | flops 2013265920 | bytes 22740992 | tf_op jit(solution)/shard_map/dot_general | solution.py:109
  72.6 0.0 slice-start.3
  72.6 0.0 slice-start.4
  72.6 11.1 %fusion.32 = bf16[96,2048]{1,0:T(8,128)(2,1)S(1)} fusion(bf16[96,5120]{1,0:T(8,128)(2,1)S(1)} %reshape.55, bf16[1,5120,2048]{2,1,0:T(8,128)(2,1)} %param.18, f32[96,2048]{1,0:T(8,128)S(1)} %fusion.24), kind=kOutput, calls=%fused_computation.31 | convolution fusion | flops 2014445568 | bytes 23134208 | tf_op jit(solution)/shard_map/dot_general | solution.py:110
  83.7 2.4 %all_gather.15 = bf16[96,4096]{1,0:T(8,128)(2,1)S(1)} all-gather(bf16[96,2048]{1,0:T(8,128)(2,1)S(1)} %fusion.32), channel_id=1, replica_groups=mesh['ctx'=16,'tp'=2] {'tp'}, dimensions={1}, use_global_device_ids=true | all-gather | bytes 1179648 | tf_op jit(solution)/shard_map/all_gather | solution.py:112
  86.2 0.0 copy-start.5
  86.2 3.4 %fusion.26 = bf16[96,2560]{1,0:T(8,128)(2,1)S(1)} fusion(bf16[96,4096]{1,0:T(8,128)(2,1)S(1)} %all_gather.15, bf16[1,4096,2560]{2,1,0:T(8,128)(2,1)S(1)} %bitcast.52), kind=kOutput, calls=%fused_computation.28 | convolution fusion | flops 2013511680 | bytes 22249472 | tf_op jit(solution)/shard_map/dot_general | solution.py:113
  89.6 0.0 copy-start.3
  89.6 1.0 reshape.56
  90.6 3.6 %all-to-all-start.1 = ((bf16[16,6,2560]{2,1,0:T(8,128)(2,1)}), bf16[16,6,2560]{2,1,0:T(8,128)(2,1)S(1)}, u32[]{:S(2)}, u32[]{:S(2)}) async-start(bf16[16,6,2560]{2,1,0:T(8,128)(2,1)} %reshape.56), calls=%async_computation.1 | async-start | bytes 1310720 | tf_op jit(solution)/shard_map/all_to_all | solution.py:117
  94.2 48.7 %all_gather.13 = bf16[1024,256]{1,0:T(8,128)(2,1)S(1)} all-gather(bf16[64,256]{1,0:T(8,128)(2,1)S(1)} %copy-done.5), channel_id=1, replica_groups=mesh['ctx'=16,'tp'=2] {'ctx'}, dimensions={0}, use_global_device_ids=true | all-gather | bytes 557056 | tf_op jit(solution)/shard_map/all_gather | solution.py:35
  142.9 6.3 %conditional.1 = ((f32[2,5,64]{2,1,0:T(8,128)S(1)}, f32[64,2,5,128]{3,0,2,1:T(8,128)S(1)})) conditional(s32[]{:T(128)} %convert_element_type.33, (f32[2,5,64]{2,1,0:T(8,128)S(1)}, f32[64,2,5,128]{3,0,2,1:T(8,128)S(1)}) %tuple.25, (s32[64]{0:T(128)S(1)}, s32[1024]{0:T(1024)S(1)}, bf16[1024,256]{1,0:T(8,128)(2,1)S(1)}, bf16[64,1280]{1,0:T(8,128)(2,1)S(1)}, ...), branch_computations={%region_2.3_spmd, %region_3.6_spmd} | conditional | flops 344295296 | bytes 22939956 | solution.py:77
  142.9 0.1 broadcast_compare_fusion
  143.0 0.2 reshape.49
  143.2 0.1 reshape.48
  143.3 0.7 fusion
  144.0 1.5 copy-done.2
  145.5 0.8 fusion.2
  146.4 0.1 reshape.50
  146.5 2.6 %fusion.9 = f32[64,2,5,128]{3,0,2,1:T(8,128)S(1)} fusion(f32[2,1024,64,5]{1,2,3,0:T(8,128)} %copy-done.2, f32[2,5,64]{2,1,0:T(8,128)S(1)} %broadcast_maximum_fusion, pred[64,1024]{1,0:T(8,128)(4,1)S(1)} %broadcast_compare_fusion, bf16[1024,2,128,1]{2,1,0,3:T(2,128)(2,1)S(1)} %bitcast.53, f32[64,2,5,128]{3,0,2,1:T(8,128)S(1)} %get-tuple-element.89, ...), kind=kOutput, calls=%fused_computation.9 | convolution fusion | flops 171212800 | bytes 3871744 | tf_op jit(solution)/shard_map/while/body/eval_jaxpr/cond/branch_1_fun/hgqk,khd->qhgd/dot_general | solution.py:65
  149.1 0.2 divide_convert_fusion
  149.3 0.1 copy.19
  149.4 0.9 convert_element_type.35
  150.3 0.0 all-to-all-done.1
  150.3 0.0 copy-start.1
  150.3 0.1 reshape.60
  150.5 0.0 copy-start.7
  150.5 0.8 gather_fusion
  151.3 0.8 multiply_convert_fusion
  (22 shorter events, 0.1 us)
Async XLA Ops:
  0.6 2.4 %copy-start = (bf16[64,2560]{1,0:T(8,128)(2,1)S(1)}, bf16[64,2560]{1,0:T(8,128)(2,1)}, u32[]{:S(2)}) copy-start(bf16[64,2560]{1,0:T(8,128)(2,1)} %param.14) | copy-start | bytes 983044
  0.6 14.6 %copy-start.4 = (bf16[64,256]{1,0:T(8,128)(2,1)S(1)}, bf16[64,256]{1,0:T(8,128)(2,1)}, u32[]{:S(2)}) copy-start(bf16[64,256]{1,0:T(8,128)(2,1)} %param.12) | copy-start | bytes 98308
  4.3 56.2 %all-to-all-start = ((bf16[16,6,2560]{2,1,0:T(8,128)(2,1)}), bf16[16,6,2560]{2,1,0:T(8,128)(2,1)S(1)}, u32[]{:S(2)}, u32[]{:S(2)}) async-start(bf16[16,6,2560]{2,1,0:T(8,128)(2,1)} %reshape_reshape.3), calls=%async_computation | async-start | bytes 1310720 | tf_op jit(solution)/shard_map/all_to_all | solution.py:105
  63.6 22.5 %slice-start = ((s8[20971520]{0:T(1024)(128)(4,1)}), s8[4194304]{0:T(1024)(128)(4,1)S(1)}, s32[]{:S(2)}) async-start(s8[20971520]{0:T(1024)(128)(4,1)} %bitcast.51), calls=%async_computation.2 | async-start | bytes 8388608
  63.6 22.5 %slice-start.1 = ((s8[20971520]{0:T(1024)(128)(4,1)}), s8[4194304]{0:T(1024)(128)(4,1)S(1)}, s32[]{:S(2)}) async-start(s8[20971520]{0:T(1024)(128)(4,1)} %bitcast.51), calls=%async_computation.3 | async-start | bytes 8388608
  63.7 22.5 %slice-start.2 = ((s8[20971520]{0:T(1024)(128)(4,1)}), s8[4194304]{0:T(1024)(128)(4,1)S(1)}, s32[]{:S(2)}) async-start(s8[20971520]{0:T(1024)(128)(4,1)} %bitcast.51), calls=%async_computation.4 | async-start | bytes 8388608
  72.6 13.5 %slice-start.3 = ((s8[20971520]{0:T(1024)(128)(4,1)}), s8[4194304]{0:T(1024)(128)(4,1)S(1)}, s32[]{:S(2)}) async-start(s8[20971520]{0:T(1024)(128)(4,1)} %bitcast.51), calls=%async_computation.5 | async-start | bytes 8388608
  72.6 13.5 %slice-start.4 = ((s8[20971520]{0:T(1024)(128)(4,1)}), s8[4194304]{0:T(1024)(128)(4,1)S(1)}, s32[]{:S(2)}) async-start(s8[20971520]{0:T(1024)(128)(4,1)} %bitcast.51), calls=%async_computation.6 | async-start | bytes 8388608
  86.2 8.1 %copy-start.5 = (bf16[64,256]{1,0:T(8,128)(2,1)S(1)}, bf16[64,256]{1,0:T(8,128)(2,1)}, u32[]{:S(2)}) copy-start(bf16[64,256]{1,0:T(8,128)(2,1)} %param.13) | copy-start | bytes 98308
  89.6 53.3 %copy-start.3 = (bf16[64,1280]{1,0:T(8,128)(2,1)S(1)}, bf16[64,1280]{1,0:T(8,128)(2,1)}, u32[]{:S(2)}) copy-start(bf16[64,1280]{1,0:T(8,128)(2,1)} %param.11) | copy-start | bytes 491524
  90.6 59.7 %all-to-all-start.1 = ((bf16[16,6,2560]{2,1,0:T(8,128)(2,1)}), bf16[16,6,2560]{2,1,0:T(8,128)(2,1)S(1)}, u32[]{:S(2)}, u32[]{:S(2)}) async-start(bf16[16,6,2560]{2,1,0:T(8,128)(2,1)} %reshape.56), calls=%async_computation.1 | async-start | bytes 1310720 | tf_op jit(solution)/shard_map/all_to_all | solution.py:117
  142.9 7.4 %copy-start.6 = (s32[64,1]{0,1:T(1,128)S(1)}, s32[64,1]{0,1:T(1,128)}, u32[]{:S(2)}) copy-start(s32[64,1]{0,1:T(1,128)} %param.15) | copy-start | bytes 772
  144.0 1.5 copy-start.2
  150.3 1.8 %copy-start.1 = (bf16[64,2560]{1,0:T(8,128)(2,1)S(1)}, bf16[64,2560]{1,0:T(8,128)(2,1)}, u32[]{:S(2)}) copy-start(bf16[64,2560]{1,0:T(8,128)(2,1)} %param.14) | copy-start | bytes 983044
  150.5 0.8 copy-start.7
where the time goes:
time: 153 us; the launch traced here: 152 us
  blocking collectives  99 us (65%)
  matrix products  27 us (18%)
  starting transfers between devices  11.9 us (8%)
  local copies, waits for them, and re-layouts  6.33 us (4%)
  other arithmetic  5.61 us (4%)
  between operations  2.2 us (1%)
    all_gather x1, blocking collectives, body(): lax.all_gather(value_use, 'ctx', axis=0, tiled=True)  48.7 us
    all_gather x1, blocking collectives, body(): lax.all_gather(key_use, 'ctx', axis=0, tiled=True)  45.2 us
    dot_general x1, matrix products, body(): up_val = jnp.dot(flat_rows, w_up[0], preferred_element_type=jnp.float32)  11.1 us
    dot_general x1, matrix products, body(): gate_val = jnp.dot(flat_rows, w_gate[0], preferred_element_type=jnp.float32)  8.92 us
    all_to_all x1, starting transfers between devices, body(): lax.all_to_all(packed, 'ctx', split_axis=0, concat_axis=0, tiled=True)  8.34 us
    all_to_all x1, starting transfers between devices, body(): lax.all_to_all(partial_out, 'ctx', split_axis=0, concat_axis=0, tiled=True)  3.59 us
    dot_general x1, matrix products, body(): jnp.dot(pair_inner, w_down[0], preferred_element_type=jnp.float32)  3.41 us
  transfers between devices with their start and end apart: 2, of which 0 were waited for; matrix products, arithmetic and copies ran while one was open for 5% of the time, Pallas kernels for 0%

commit v1 on v0

--- a/solution.py
+++ b/solution.py
@@ -8,6 +8,28 @@
 EXPERTS = 16
 CAP = 6
 masked_score = -1e30
+
+
+def in_blocks(x, dim, count):
+    before, after = (x.shape[:dim], x.shape[dim + 1 :])
+    return jnp.moveaxis(x.reshape(*before, count, -1, *after), dim, 0)
+
+
+def in_order(blocks, dim):
+    blocks = jnp.moveaxis(blocks, 0, dim)
+    dims = blocks.shape
+    return blocks.reshape(*dims[:dim], dims[dim] * dims[dim + 1], *dims[dim + 2 :])
+
+
+def exchange_directly(x, axis, split_dim, concat_dim):
+    devices, index = (lax.axis_size(axis), lax.axis_index(axis))
+    pieces = in_blocks(x, split_dim, devices)
+    done = [pieces[index]]
+    for lap in range(1, devices):
+        sent = pieces[(index + lap) % devices]
+        done.append(lax.ppermute(sent, axis, [(i, (i + lap) % devices) for i in range(devices)]))
+    pieces = jnp.stack(done)[(index - jnp.arange(devices)) % devices]
+    return in_order(pieces, concat_dim)
 
 
 def body(
@@ -102,7 +124,7 @@
     packed = jnp.broadcast_to(
         packed.reshape(EXPERTS, 1, CAP, feature_width), (EXPERTS, host_count, CAP, feature_width)
     ).reshape(ctx_count, CAP, feature_width)
-    arrived = lax.all_to_all(packed, "ctx", split_axis=0, concat_axis=0, tiled=True)
+    arrived = exchange_directly(packed, "ctx", 0, 0)
     arrived = lax.all_gather(arrived, "tp", axis=2, tiled=True)
     slot_count = arrived.shape[1]
     flat_rows = arrived.reshape(-1, arrived.shape[2])

time: 153 us -> 173 us (1.13)
  starting transfers between devices: 11.9 us -> 33.4 us
  blocking collectives: 99 us -> 96.3 us
    ppermute x0 -> x15, starting transfers between devices: none -> 26.1 us  [exchange_directly(): lax.ppermute(sent, axis, [(i, (i + lap) % devices) for i in range(devices)])]
    all_to_all x1 -> x0, starting transfers between devices: 8.34 us -> none  [body(): lax.all_to_all(packed, 'ctx', split_axis=0, concat_axis=0, tiled=True)]
    all_to_all x1, starting transfers between devices: 3.59 us -> 7.3 us  [body(): lax.all_to_all(partial_out, 'ctx', split_axis=0, concat_axis=0, tiled=True)]
    all_gather x1, blocking collectives: 45.2 us -> 42.9 us  [body(): lax.all_gather(key_use, 'ctx', axis=0, tiled=True)]
  transfers between devices with their start and end apart: 2 -> 16, of which waited for: 0 -> 2; matrix products, arithmetic and copies ran while one was open for 5% -> 4% of each run, Pallas kernels for 0% -> 0%
where the time goes in v1:
time: 173 us
  blocking collectives  96.3 us (56%)
  starting transfers between devices  33.4 us (19%)
  matrix products  27 us (16%)
  local copies, waits for them, and re-layouts  6.24 us (4%)
  other arithmetic  5.58 us (3%)
  between operations  2.57 us (1%)
    all_gather x1, blocking collectives, body(): lax.all_gather(value_use, 'ctx', axis=0, tiled=True)  48.3 us
    all_gather x1, blocking collectives, body(): lax.all_gather(key_use, 'ctx', axis=0, tiled=True)  42.9 us
    ppermute x15, starting transfers between devices, exchange_directly(): lax.ppermute(sent, axis, [(i, (i + lap) % devices) for i in range(devices)])  26.1 us
    dot_general x1, matrix products, body(): up_val = jnp.dot(flat_rows, w_up[0], preferred_element_type=jnp.float32)  11.1 us
    dot_general x1, matrix products, body(): gate_val = jnp.dot(flat_rows, w_gate[0], preferred_element_type=jnp.float32)  8.92 us
    all_to_all x1, starting transfers between devices, body(): lax.all_to_all(partial_out, 'ctx', split_axis=0, concat_axis=0, tiled=True)  7.3 us
  transfers between devices with their start and end apart: 16, of which 2 were waited for; matrix products, arithmetic and copies ran while one was open for 4% of the time, Pallas kernels for 0%

profile of v1, /device:TPU:0, one launch (start us, length us, event | category | flops | bytes accessed | tf_op | source)
XLA Modules:
  0.0 172.9 jit_solution(16283771299741209871)
XLA Ops:
  0.8 0.7 fusion.35
  1.7 0.8 select_reduce_fusion
  2.5 0.7 multiply_add_fusion.1
  3.2 0.3 convolution_convert_fusion
  3.4 0.2 reshape_reshape_reshape.3
  3.7 0.1 dynamic-slice_bitcast_fusion
  3.8 3.0 %collective-permute-start = (bf16[1,6,2560]{2,1,0:T(8,128)(2,1)S(1)}, bf16[1,6,2560]{2,1,0:T(8,128)(2,1)S(1)}, u32[]{:S(2)}, u32[]{:S(2)}) collective-permute-start(bf16[1,6,2560]{2,1,0:T(8,128)(2,1)S(1)} %get-tuple-element.117), channel_id=1, source_target_pairs={{0,2},{2,4},{4,6},{6,8},{8,10},{10,12},{12,14},{14,16},{16,18},{18... | collective-permute-start | bytes 92168 | tf_op jit(solution)/shard_map/ppermute | solution.py:30
  6.8 1.5 collective-permute-start.1
  8.4 2.4 %collective-permute-start.2 = (bf16[1,6,2560]{2,1,0:T(8,128)(2,1)S(1)}, bf16[1,6,2560]{2,1,0:T(8,128)(2,1)S(1)}, u32[]{:S(2)}, u32[]{:S(2)}) collective-permute-start(bf16[1,6,2560]{2,1,0:T(8,128)(2,1)S(1)} %get-tuple-element.115), channel_id=1, source_target_pairs={{0,6},{2,8},{4,10},{6,12},{8,14},{10,16},{12,18},{14,20},{16,22},{... | collective-permute-start | bytes 92168 | tf_op jit(solution)/shard_map/ppermute | solution.py:30
  10.8 1.6 collective-permute-start.3
  12.4 1.6 collective-permute-start.4
  14.0 42.9 %all_gather.12 = bf16[1024,256]{1,0:T(8,128)(2,1)S(1)} all-gather(bf16[64,256]{1,0:T(8,128)(2,1)S(1)} %copy-done.4), channel_id=1, replica_groups=mesh['ctx'=16,'tp'=2] {'ctx'}, dimensions={0}, use_global_device_ids=true | all-gather | bytes 557056 | tf_op jit(solution)/shard_map/all_gather | solution.py:56
  57.0 0.6 fusion.50
  57.6 0.6 fusion.46
  59.8 0.2 collective-permute-start.7
  60.0 3.6 %collective-permute-start.8 = (bf16[1,6,2560]{2,1,0:T(8,128)(2,1)S(1)}, bf16[1,6,2560]{2,1,0:T(8,128)(2,1)S(1)}, u32[]{:S(2)}, u32[]{:S(2)}) collective-permute-start(bf16[1,6,2560]{2,1,0:T(8,128)(2,1)S(1)} %get-tuple-element.109), channel_id=1, source_target_pairs={{0,18},{2,20},{4,22},{6,24},{8,26},{10,28},{12,30},{14,0},{16,2},{... | collective-permute-start | bytes 92168 | tf_op jit(solution)/shard_map/ppermute | solution.py:30
  63.6 3.7 %collective-permute-start.9 = (bf16[1,6,2560]{2,1,0:T(8,128)(2,1)S(1)}, bf16[1,6,2560]{2,1,0:T(8,128)(2,1)S(1)}, u32[]{:S(2)}, u32[]{:S(2)}) collective-permute-start(bf16[1,6,2560]{2,1,0:T(8,128)(2,1)S(1)} %get-tuple-element.108), channel_id=1, source_target_pairs={{0,20},{2,22},{4,24},{6,26},{8,28},{10,30},{12,0},{14,2},{16,4},{1... | collective-permute-start | bytes 92168 | tf_op jit(solution)/shard_map/ppermute | solution.py:30
  67.5 2.5 %collective-permute-start.11 = (bf16[1,6,2560]{2,1,0:T(8,128)(2,1)S(1)}, bf16[1,6,2560]{2,1,0:T(8,128)(2,1)S(1)}, u32[]{:S(2)}, u32[]{:S(2)}) collective-permute-start(bf16[1,6,2560]{2,1,0:T(8,128)(2,1)S(1)} %get-tuple-element.106), channel_id=1, source_target_pairs={{0,24},{2,26},{4,28},{6,30},{8,0},{10,2},{12,4},{14,6},{16,8},{18,... | collective-permute-start | bytes 92168 | tf_op jit(solution)/shard_map/ppermute | solution.py:30
  70.0 2.7 %collective-permute-start.12 = (bf16[1,6,2560]{2,1,0:T(8,128)(2,1)S(1)}, bf16[1,6,2560]{2,1,0:T(8,128)(2,1)S(1)}, u32[]{:S(2)}, u32[]{:S(2)}) collective-permute-start(bf16[1,6,2560]{2,1,0:T(8,128)(2,1)S(1)} %get-tuple-element.105), channel_id=1, source_target_pairs={{0,26},{2,28},{4,30},{6,0},{8,2},{10,4},{12,6},{14,8},{16,10},{18,... | collective-permute-start | bytes 92168 | tf_op jit(solution)/shard_map/ppermute | solution.py:30
  72.7 0.6 collective-permute-start.13
  73.3 2.4 %collective-permute-start.14 = (bf16[1,6,2560]{2,1,0:T(8,128)(2,1)S(1)}, bf16[1,6,2560]{2,1,0:T(8,128)(2,1)S(1)}, u32[]{:S(2)}, u32[]{:S(2)}) collective-permute-start(bf16[1,6,2560]{2,1,0:T(8,128)(2,1)S(1)} %get-tuple-element.103), channel_id=1, source_target_pairs={{0,30},{2,0},{4,2},{6,4},{8,6},{10,8},{12,10},{14,12},{16,14},{18,... | collective-permute-start | bytes 92168 | tf_op jit(solution)/shard_map/ppermute | solution.py:30
  75.7 1.0 collective-permute-done.13
  76.7 0.6 collective-permute-done.14
  77.3 0.6 gather_fusion
  77.9 2.7 %all-gather = bf16[16,6,5120]{2,1,0:T(8,128)(2,1)S(1)} all-gather(bf16[16,6,2560]{2,1,0:T(8,128)(2,1)S(1)} %gather_fusion), channel_id=2, replica_groups=mesh['ctx'=16,'tp'=2] {'tp'}, dimensions={2}, use_global_device_ids=true | all-gather | bytes 1474560 | tf_op jit(solution)/shard_map/all_gather | solution.py:128
  80.7 0.4 reshape.108
  81.1 8.9 %fusion.24 = f32[96,2048]{1,0:T(8,128)S(1)} fusion(bf16[96,5120]{1,0:T(8,128)(2,1)S(1)} %reshape.108, bf16[1,5120,2048]{2,1,0:T(8,128)(2,1)} %param.17), kind=kOutput, calls=%fused_computation.27 | convolution fusion | flops 2013265920 | bytes 22740992 | tf_op jit(solution)/shard_map/dot_general | solution.py:131
  90.0 11.1 %fusion.32 = bf16[96,2048]{1,0:T(8,128)(2,1)S(1)} fusion(bf16[96,5120]{1,0:T(8,128)(2,1)S(1)} %reshape.108, bf16[1,5120,2048]{2,1,0:T(8,128)(2,1)} %param.18, f32[96,2048]{1,0:T(8,128)S(1)} %fusion.24), kind=kOutput, calls=%fused_computation.32 | convolution fusion | flops 2014445568 | bytes 23134208 | tf_op jit(solution)/shard_map/dot_general | solution.py:132
  101.1 2.4 %all_gather.15 = bf16[96,4096]{1,0:T(8,128)(2,1)S(1)} all-gather(bf16[96,2048]{1,0:T(8,128)(2,1)S(1)} %fusion.32), channel_id=1, replica_groups=mesh['ctx'=16,'tp'=2] {'tp'}, dimensions={1}, use_global_device_ids=true | all-gather | bytes 1179648 | tf_op jit(solution)/shard_map/all_gather | solution.py:134
  103.6 3.4 %fusion.26 = bf16[96,2560]{1,0:T(8,128)(2,1)S(1)} fusion(bf16[96,4096]{1,0:T(8,128)(2,1)S(1)} %all_gather.15, bf16[1,4096,2560]{2,1,0:T(8,128)(2,1)S(1)} %bitcast.115), kind=kOutput, calls=%fused_computation.29 | convolution fusion | flops 2013511680 | bytes 22249472 | tf_op jit(solution)/shard_map/dot_general | solution.py:135
  107.0 1.0 reshape.109
  108.0 7.3 %all-to-all-start = ((bf16[16,6,2560]{2,1,0:T(8,128)(2,1)}), bf16[16,6,2560]{2,1,0:T(8,128)(2,1)S(1)}, u32[]{:S(2)}, u32[]{:S(2)}) async-start(bf16[16,6,2560]{2,1,0:T(8,128)(2,1)} %reshape.109), calls=%async_computation | async-start | bytes 1310720 | tf_op jit(solution)/shard_map/all_to_all | solution.py:139
  115.3 48.3 %all_gather.13 = bf16[1024,256]{1,0:T(8,128)(2,1)S(1)} all-gather(bf16[64,256]{1,0:T(8,128)(2,1)S(1)} %copy-done.5), channel_id=1, replica_groups=mesh['ctx'=16,'tp'=2] {'ctx'}, dimensions={0}, use_global_device_ids=true | all-gather | bytes 557056 | tf_op jit(solution)/shard_map/all_gather | solution.py:57
  163.6 6.2 %conditional.1 = ((f32[2,5,64]{2,1,0:T(8,128)S(1)}, f32[64,2,5,128]{3,0,2,1:T(8,128)S(1)})) conditional(s32[]{:T(128)} %convert_element_type.33, (f32[2,5,64]{2,1,0:T(8,128)S(1)}, f32[64,2,5,128]{3,0,2,1:T(8,128)S(1)}) %tuple.25, (s32[64]{0:T(128)S(1)}, s32[1024]{0:T(1024)S(1)}, bf16[1024,256]{1,0:T(8,128)(2,1)S(1)}, bf16[64,1280]{1,0:T(8,128)(2,1)S(1)}, ...), branch_computations={%region_2.3_spmd, %region_3.6_spmd} | conditional | flops 344295296 | bytes 22939956 | solution.py:99
  163.6 0.1 broadcast_compare_fusion
  163.7 0.2 reshape.100
  163.9 0.1 reshape.99
  164.1 0.7 fusion
  164.8 1.5 copy-done.2
  166.3 0.8 fusion.2
  167.1 0.1 reshape.101
  167.2 2.6 %fusion.9 = f32[64,2,5,128]{3,0,2,1:T(8,128)S(1)} fusion(f32[2,1024,64,5]{1,2,3,0:T(8,128)} %copy-done.2, f32[2,5,64]{2,1,0:T(8,128)S(1)} %broadcast_maximum_fusion, pred[64,1024]{1,0:T(8,128)(4,1)S(1)} %broadcast_compare_fusion, bf16[1024,2,128,1]{2,1,0,3:T(2,128)(2,1)S(1)} %bitcast.117, f32[64,2,5,128]{3,0,2,1:T(8,128)S(1)} %get-tuple-element.89, ...), kind=kOutput, calls=%fused_computation.10 | convolution fusion | flops 171212800 | bytes 3871744 | tf_op jit(solution)/shard_map/while/body/eval_jaxpr/cond/branch_1_fun/hgqk,khd->qhgd/dot_general | solution.py:87
  169.9 0.2 divide_convert_fusion
  170.0 0.1 copy.19
  170.2 0.9 convert_element_type.35
  171.1 0.1 reshape.113
  171.2 0.8 gather_fusion.1
  172.0 0.8 multiply_convert_fusion
  (69 shorter events, 0.6 us)
Async XLA Ops:
  0.6 2.5 %copy-start = (bf16[64,2560]{1,0:T(8,128)(2,1)S(1)}, bf16[64,2560]{1,0:T(8,128)(2,1)}, u32[]{:S(2)}) copy-start(bf16[64,2560]{1,0:T(8,128)(2,1)} %param.14) | copy-start | bytes 983044
  0.6 13.4 %copy-start.4 = (bf16[64,256]{1,0:T(8,128)(2,1)S(1)}, bf16[64,256]{1,0:T(8,128)(2,1)}, u32[]{:S(2)}) copy-start(bf16[64,256]{1,0:T(8,128)(2,1)} %param.12) | copy-start | bytes 98308
  3.8 55.8 %collective-permute-start = (bf16[1,6,2560]{2,1,0:T(8,128)(2,1)S(1)}, bf16[1,6,2560]{2,1,0:T(8,128)(2,1)S(1)}, u32[]{:S(2)}, u32[]{:S(2)}) collective-permute-start(bf16[1,6,2560]{2,1,0:T(8,128)(2,1)S(1)} %get-tuple-element.117), channel_id=1, source_target_pairs={{0,2},{2,4},{4,6},{6,8},{8,10},{10,12},{12,14},{14,16},{16,18},{18... | collective-permute-start | bytes 92168 | tf_op jit(solution)/shard_map/ppermute | solution.py:30
  6.8 52.8 %collective-permute-start.1 = (bf16[1,6,2560]{2,1,0:T(8,128)(2,1)S(1)}, bf16[1,6,2560]{2,1,0:T(8,128)(2,1)S(1)}, u32[]{:S(2)}, u32[]{:S(2)}) collective-permute-start(bf16[1,6,2560]{2,1,0:T(8,128)(2,1)S(1)} %get-tuple-element.116), channel_id=1, source_target_pairs={{0,4},{2,6},{4,8},{6,10},{8,12},{10,14},{12,16},{14,18},{16,20},{1... | collective-permute-start | bytes 92168 | tf_op jit(solution)/shard_map/ppermute | solution.py:30
  8.4 51.4 %collective-permute-start.2 = (bf16[1,6,2560]{2,1,0:T(8,128)(2,1)S(1)}, bf16[1,6,2560]{2,1,0:T(8,128)(2,1)S(1)}, u32[]{:S(2)}, u32[]{:S(2)}) collective-permute-start(bf16[1,6,2560]{2,1,0:T(8,128)(2,1)S(1)} %get-tuple-element.115), channel_id=1, source_target_pairs={{0,6},{2,8},{4,10},{6,12},{8,14},{10,16},{12,18},{14,20},{16,22},{... | collective-permute-start | bytes 92168 | tf_op jit(solution)/shard_map/ppermute | solution.py:30
  10.8 49.2 %collective-permute-start.3 = (bf16[1,6,2560]{2,1,0:T(8,128)(2,1)S(1)}, bf16[1,6,2560]{2,1,0:T(8,128)(2,1)S(1)}, u32[]{:S(2)}, u32[]{:S(2)}) collective-permute-start(bf16[1,6,2560]{2,1,0:T(8,128)(2,1)S(1)} %get-tuple-element.114), channel_id=1, source_target_pairs={{0,8},{2,10},{4,12},{6,14},{8,16},{10,18},{12,20},{14,22},{16,24},... | collective-permute-start | bytes 92168 | tf_op jit(solution)/shard_map/ppermute | solution.py:30
  12.4 51.3 %collective-permute-start.4 = (bf16[1,6,2560]{2,1,0:T(8,128)(2,1)S(1)}, bf16[1,6,2560]{2,1,0:T(8,128)(2,1)S(1)}, u32[]{:S(2)}, u32[]{:S(2)}) collective-permute-start(bf16[1,6,2560]{2,1,0:T(8,128)(2,1)S(1)} %get-tuple-element.113), channel_id=1, source_target_pairs={{0,10},{2,12},{4,14},{6,16},{8,18},{10,20},{12,22},{14,24},{16,26}... | collective-permute-start | bytes 92168 | tf_op jit(solution)/shard_map/ppermute | solution.py:30
  59.6 7.8 %collective-permute-start.5 = (bf16[1,6,2560]{2,1,0:T(8,128)(2,1)S(1)}, bf16[1,6,2560]{2,1,0:T(8,128)(2,1)S(1)}, u32[]{:S(2)}, u32[]{:S(2)}) collective-permute-start(bf16[1,6,2560]{2,1,0:T(8,128)(2,1)S(1)} %get-tuple-element.112), channel_id=1, source_target_pairs={{0,12},{2,14},{4,16},{6,18},{8,20},{10,22},{12,24},{14,26},{16,28}... | collective-permute-start | bytes 92168 | tf_op jit(solution)/shard_map/ppermute | solution.py:30
  59.7 7.8 %collective-permute-start.6 = (bf16[1,6,2560]{2,1,0:T(8,128)(2,1)S(1)}, bf16[1,6,2560]{2,1,0:T(8,128)(2,1)S(1)}, u32[]{:S(2)}, u32[]{:S(2)}) collective-permute-start(bf16[1,6,2560]{2,1,0:T(8,128)(2,1)S(1)} %get-tuple-element.111), channel_id=1, source_target_pairs={{0,14},{2,16},{4,18},{6,20},{8,22},{10,24},{12,26},{14,28},{16,30}... | collective-permute-start | bytes 92168 | tf_op jit(solution)/shard_map/ppermute | solution.py:30
  59.8 10.2 %collective-permute-start.7 = (bf16[1,6,2560]{2,1,0:T(8,128)(2,1)S(1)}, bf16[1,6,2560]{2,1,0:T(8,128)(2,1)S(1)}, u32[]{:S(2)}, u32[]{:S(2)}) collective-permute-start(bf16[1,6,2560]{2,1,0:T(8,128)(2,1)S(1)} %get-tuple-element.110), channel_id=1, source_target_pairs={{0,16},{2,18},{4,20},{6,22},{8,24},{10,26},{12,28},{14,30},{16,0},... | collective-permute-start | bytes 92168 | tf_op jit(solution)/shard_map/ppermute | solution.py:30
  60.0 12.7 %collective-permute-start.8 = (bf16[1,6,2560]{2,1,0:T(8,128)(2,1)S(1)}, bf16[1,6,2560]{2,1,0:T(8,128)(2,1)S(1)}, u32[]{:S(2)}, u32[]{:S(2)}) collective-permute-start(bf16[1,6,2560]{2,1,0:T(8,128)(2,1)S(1)} %get-tuple-element.109), channel_id=1, source_target_pairs={{0,18},{2,20},{4,22},{6,24},{8,26},{10,28},{12,30},{14,0},{16,2},{... | collective-permute-start | bytes 92168 | tf_op jit(solution)/shard_map/ppermute | solution.py:30
  63.6 9.6 %collective-permute-start.9 = (bf16[1,6,2560]{2,1,0:T(8,128)(2,1)S(1)}, bf16[1,6,2560]{2,1,0:T(8,128)(2,1)S(1)}, u32[]{:S(2)}, u32[]{:S(2)}) collective-permute-start(bf16[1,6,2560]{2,1,0:T(8,128)(2,1)S(1)} %get-tuple-element.108), channel_id=1, source_target_pairs={{0,20},{2,22},{4,24},{6,26},{8,28},{10,30},{12,0},{14,2},{16,4},{1... | collective-permute-start | bytes 92168 | tf_op jit(solution)/shard_map/ppermute | solution.py:30
  67.4 8.3 %collective-permute-start.10 = (bf16[1,6,2560]{2,1,0:T(8,128)(2,1)S(1)}, bf16[1,6,2560]{2,1,0:T(8,128)(2,1)S(1)}, u32[]{:S(2)}, u32[]{:S(2)}) collective-permute-start(bf16[1,6,2560]{2,1,0:T(8,128)(2,1)S(1)} %get-tuple-element.107), channel_id=1, source_target_pairs={{0,22},{2,24},{4,26},{6,28},{8,30},{10,0},{12,2},{14,4},{16,6},{18... | collective-permute-start | bytes 92168 | tf_op jit(solution)/shard_map/ppermute | solution.py:30
  67.5 8.2 %collective-permute-start.11 = (bf16[1,6,2560]{2,1,0:T(8,128)(2,1)S(1)}, bf16[1,6,2560]{2,1,0:T(8,128)(2,1)S(1)}, u32[]{:S(2)}, u32[]{:S(2)}) collective-permute-start(bf16[1,6,2560]{2,1,0:T(8,128)(2,1)S(1)} %get-tuple-element.106), channel_id=1, source_target_pairs={{0,24},{2,26},{4,28},{6,30},{8,0},{10,2},{12,4},{14,6},{16,8},{18,... | collective-permute-start | bytes 92168 | tf_op jit(solution)/shard_map/ppermute | solution.py:30
  70.0 5.7 %collective-permute-start.12 = (bf16[1,6,2560]{2,1,0:T(8,128)(2,1)S(1)}, bf16[1,6,2560]{2,1,0:T(8,128)(2,1)S(1)}, u32[]{:S(2)}, u32[]{:S(2)}) collective-permute-start(bf16[1,6,2560]{2,1,0:T(8,128)(2,1)S(1)} %get-tuple-element.105), channel_id=1, source_target_pairs={{0,26},{2,28},{4,30},{6,0},{8,2},{10,4},{12,6},{14,8},{16,10},{18,... | collective-permute-start | bytes 92168 | tf_op jit(solution)/shard_map/ppermute | solution.py:30
  72.7 4.0 %collective-permute-start.13 = (bf16[1,6,2560]{2,1,0:T(8,128)(2,1)S(1)}, bf16[1,6,2560]{2,1,0:T(8,128)(2,1)S(1)}, u32[]{:S(2)}, u32[]{:S(2)}) collective-permute-start(bf16[1,6,2560]{2,1,0:T(8,128)(2,1)S(1)} %get-tuple-element.104), channel_id=1, source_target_pairs={{0,28},{2,30},{4,0},{6,2},{8,4},{10,6},{12,8},{14,10},{16,12},{18,... | collective-permute-start | bytes 92168 | tf_op jit(solution)/shard_map/ppermute | solution.py:30
  73.3 4.0 %collective-permute-start.14 = (bf16[1,6,2560]{2,1,0:T(8,128)(2,1)S(1)}, bf16[1,6,2560]{2,1,0:T(8,128)(2,1)S(1)}, u32[]{:S(2)}, u32[]{:S(2)}) collective-permute-start(bf16[1,6,2560]{2,1,0:T(8,128)(2,1)S(1)} %get-tuple-element.103), channel_id=1, source_target_pairs={{0,30},{2,0},{4,2},{6,4},{8,6},{10,8},{12,10},{14,12},{16,14},{18,... | collective-permute-start | bytes 92168 | tf_op jit(solution)/shard_map/ppermute | solution.py:30
  81.0 22.5 %slice-start = ((s8[20971520]{0:T(1024)(128)(4,1)}), s8[4194304]{0:T(1024)(128)(4,1)S(1)}, s32[]{:S(2)}) async-start(s8[20971520]{0:T(1024)(128)(4,1)} %bitcast.114), calls=%async_computation.1 | async-start | bytes 8388608
  81.0 22.5 %slice-start.1 = ((s8[20971520]{0:T(1024)(128)(4,1)}), s8[4194304]{0:T(1024)(128)(4,1)S(1)}, s32[]{:S(2)}) async-start(s8[20971520]{0:T(1024)(128)(4,1)} %bitcast.114), calls=%async_computation.2 | async-start | bytes 8388608
  81.1 22.5 %slice-start.2 = ((s8[20971520]{0:T(1024)(128)(4,1)}), s8[4194304]{0:T(1024)(128)(4,1)S(1)}, s32[]{:S(2)}) async-start(s8[20971520]{0:T(1024)(128)(4,1)} %bitcast.114), calls=%async_computation.3 | async-start | bytes 8388608
  90.0 13.5 %slice-start.3 = ((s8[20971520]{0:T(1024)(128)(4,1)}), s8[4194304]{0:T(1024)(128)(4,1)S(1)}, s32[]{:S(2)}) async-start(s8[20971520]{0:T(1024)(128)(4,1)} %bitcast.114), calls=%async_computation.4 | async-start | bytes 8388608
  90.0 13.5 %slice-start.4 = ((s8[20971520]{0:T(1024)(128)(4,1)}), s8[4194304]{0:T(1024)(128)(4,1)S(1)}, s32[]{:S(2)}) async-start(s8[20971520]{0:T(1024)(128)(4,1)} %bitcast.114), calls=%async_computation.5 | async-start | bytes 8388608
  103.6 11.8 %copy-start.5 = (bf16[64,256]{1,0:T(8,128)(2,1)S(1)}, bf16[64,256]{1,0:T(8,128)(2,1)}, u32[]{:S(2)}) copy-start(bf16[64,256]{1,0:T(8,128)(2,1)} %param.13) | copy-start | bytes 98308
  107.0 56.6 %copy-start.3 = (bf16[64,1280]{1,0:T(8,128)(2,1)S(1)}, bf16[64,1280]{1,0:T(8,128)(2,1)}, u32[]{:S(2)}) copy-start(bf16[64,1280]{1,0:T(8,128)(2,1)} %param.11) | copy-start | bytes 491524
  108.0 63.1 %all-to-all-start = ((bf16[16,6,2560]{2,1,0:T(8,128)(2,1)}), bf16[16,6,2560]{2,1,0:T(8,128)(2,1)S(1)}, u32[]{:S(2)}, u32[]{:S(2)}) async-start(bf16[16,6,2560]{2,1,0:T(8,128)(2,1)} %reshape.109), calls=%async_computation | async-start | bytes 1310720 | tf_op jit(solution)/shard_map/all_to_all | solution.py:139
  163.6 7.4 %copy-start.6 = (s32[64,1]{0,1:T(1,128)S(1)}, s32[64,1]{0,1:T(1,128)}, u32[]{:S(2)}) copy-start(s32[64,1]{0,1:T(1,128)} %param.15) | copy-start | bytes 772
  164.8 1.5 copy-start.2
  171.0 1.8 %copy-start.1 = (bf16[64,2560]{1,0:T(8,128)(2,1)S(1)}, bf16[64,2560]{1,0:T(8,128)(2,1)}, u32[]{:S(2)}) copy-start(bf16[64,2560]{1,0:T(8,128)(2,1)} %param.14) | copy-start | bytes 983044
  171.2 0.8 copy-start.7
